TPU v7x, 32 devices: a whole 2x2x4 slice. The times are simulated.
32 devices in a mesh: tensor: 4 (over z), dp: 8 (over y, x, core).
Axes of the slice: x: 2, y: 2, z: 4, core: 2. Of those that a mesh axis runs over, the one named last changes fastest.
Arguments:
- grads: bfloat16 [8, 40, 28672], P('dp', None, 'tensor'), may hold values from -6 to 6
- offload_mask: int32 [8, 5], replicated, may hold values from 0 to 1, as said below
- owner_map: int32 [8], replicated, may hold values from 0 to 7, as said below
- local_master: float32 [24, 28672], P('dp', 'tensor'), may hold values from -6 to 6
- local_moment: float32 [24, 28672], P('dp', 'tensor'), may hold values from -1.2 to 1.2
- local_second: float32 [24, 28672], P('dp', 'tensor'), may hold values from 0.001 to 0.1
- offload_master: float32 [16, 2, 28672], P('dp', None, 'tensor'), may hold values from -6 to 6
- offload_moment: float32 [16, 2, 28672], P('dp', None, 'tensor'), may hold values from -1.2 to 1.2
- offload_second: float32 [16, 2, 28672], P('dp', None, 'tensor'), may hold values from 0.001 to 0.1
Outputs:
- new_weights: bfloat16 [40, 28672], P(None, 'tensor')
- grad_norm: float32 [], replicated
- new_local_master: float32 [24, 28672], P('dp', 'tensor')
- new_local_moment: float32 [24, 28672], P('dp', 'tensor')
- new_local_second: float32 [24, 28672], P('dp', 'tensor')
- new_offload_master: float32 [16, 2, 28672], P('dp', None, 'tensor')
- new_offload_moment: float32 [16, 2, 28672], P('dp', None, 'tensor')
- new_offload_second: float32 [16, 2, 28672], P('dp', None, 'tensor')
Inputs may be any that keep to these rules, and one draw needn't show every extreme that they name: Each row of offload_mask holds exactly 2 ones. `owner_map`: no device is named by more than 2 shards, and some device is named by exactly 2.
All inputs are finite; a program needn't handle non-finite values.
Results may differ from a plain program's by a relative error of at most 0.0039.
Values may be sent and summed in bfloat16 or wider, within the bound.
A program may use at most 128 MiB of HBM per device.

v0:
```python
import jax
import jax.numpy as jnp
from jax import lax
from jax.sharding import PartitionSpec as P

beta_first = 0.9
beta_second = 0.95
learn_rate = 0.02
decay_rate = 0.1
epsilon_value = 1e-08
step_count = 10
bias_first = 1.0 - beta_first**step_count
bias_second = 1.0 - beta_second**step_count


def adam_update(master, moment, second, gradient):
    moment_new = beta_first * moment + (1.0 - beta_first) * gradient
    second_new = beta_second * second + (1.0 - beta_second) * gradient * gradient
    scaled = moment_new / bias_first / (jnp.sqrt(second_new / bias_second) + epsilon_value)
    master_new = master - learn_rate * (scaled + decay_rate * master)
    return (master_new, moment_new, second_new)


def row_tables(offload_mask, owner_map):
    shards = owner_map.shape[0]
    row_dev = offload_mask.shape[1]
    numbers = jnp.arange(shards, dtype=jnp.int32)
    same_owner = owner_map[:, None] == owner_map[None, :]
    earlier = numbers[None, :] < numbers[:, None]
    slot_of = jnp.sum((same_owner & earlier).astype(jnp.int32), axis=1)
    off_rank = jnp.cumsum(offload_mask, axis=1) - offload_mask
    keep_rank = jnp.arange(row_dev, dtype=jnp.int32)[None, :] - off_rank
    return (slot_of, off_rank, keep_rank)


def body(
    grads,
    offload_mask,
    owner_map,
    local_master,
    local_moment,
    local_second,
    offload_master,
    offload_moment,
    offload_second,
):
    devices = lax.axis_size("dp")
    position = lax.axis_index("dp")
    row_dev = offload_mask.shape[1]
    kept_count = local_master.shape[0]
    slot_count = offload_master.shape[0]
    offloaded = offload_master.shape[1]
    columns = grads.shape[2]
    slot_of, off_rank, keep_rank = row_tables(offload_mask, owner_map)
    is_off = offload_mask == 1
    row_range = jnp.arange(row_dev, dtype=jnp.int32)[None, None, :]
    off_hits = is_off[:, None, :] & (
        off_rank[:, None, :] == jnp.arange(offloaded, dtype=jnp.int32)[None, :, None]
    )
    off_index = jnp.sum(jnp.where(off_hits, row_range, 0), axis=2)
    keep_hits = ~is_off[:, None, :] & (
        keep_rank[:, None, :] == jnp.arange(kept_count, dtype=jnp.int32)[None, :, None]
    )
    keep_index = jnp.sum(jnp.where(keep_hits, row_range, 0), axis=2)
    shard_numbers = jnp.arange(devices, dtype=jnp.int32)
    matches = (owner_map[None, None, :] == shard_numbers[:, None, None]) & (
        slot_of[None, None, :] == jnp.arange(slot_count, dtype=jnp.int32)[None, :, None]
    )
    source_of = jnp.sum(jnp.where(matches, shard_numbers[None, None, :], 0), axis=2)
    filled = jnp.any(matches, axis=2)
    my_filled = jnp.take(filled, position, axis=0)
    local_grads = grads[0]
    keep_rows = shard_numbers[:, None] * row_dev + keep_index
    slot_rows = source_of[:, :, None] * row_dev + jnp.take(off_index, source_of, axis=0)
    row_table = jnp.concatenate(
        [keep_rows, slot_rows.reshape(devices, slot_count * offloaded)], axis=1
    ).reshape(-1)
    row_weights = jnp.concatenate(
        [
            jnp.ones((devices, kept_count), jnp.float32),
            jnp.repeat(filled.astype(jnp.float32), offloaded, axis=1),
        ],
        axis=1,
    ).reshape(-1)
    my_grads = (
        lax.psum_scatter(
            jnp.take(local_grads, row_table, axis=0).astype(jnp.float32) * row_weights[:, None],
            "dp",
            scatter_dimension=0,
            tiled=True,
        )
        / devices
    )
    keep_grad = my_grads[:kept_count]
    slot_grad = my_grads[kept_count:].reshape(slot_count, offloaded, columns)
    partial_value = jnp.sum(my_grads * my_grads)
    grad_norm = jnp.sqrt(lax.psum(partial_value, ("tensor", "dp")))
    new_local = adam_update(local_master, local_moment, local_second, keep_grad)
    updated = adam_update(offload_master, offload_moment, offload_second, slot_grad)
    formers = (offload_master, offload_moment, offload_second)
    slot_mask = my_filled[:, None, None]
    new_off = tuple((jnp.where(slot_mask, updated[place], formers[place]) for place in range(3)))
    keep_bf = new_local[0].astype(jnp.bfloat16)
    slot_bf = new_off[0].astype(jnp.bfloat16)
    back_out = jnp.where(
        (owner_map == position)[:, None, None],
        jnp.take(slot_bf, slot_of, axis=0),
        jnp.zeros((), jnp.bfloat16),
    )
    back_in = lax.all_to_all(back_out, "dp", split_axis=0, concat_axis=0, tiled=True)
    mine_off = jnp.take(back_in, jnp.take(owner_map, position), axis=0)
    stacked = jnp.concatenate([keep_bf, mine_off], axis=0)
    order_rows = jnp.where(
        jnp.take(is_off, position, axis=0),
        kept_count + jnp.take(off_rank, position, axis=0),
        jnp.take(keep_rank, position, axis=0),
    )
    new_weights = lax.all_gather(jnp.take(stacked, order_rows, axis=0), "dp", axis=0, tiled=True)
    return (
        new_weights,
        grad_norm,
        new_local[0],
        new_local[1],
        new_local[2],
        new_off[0],
        new_off[1],
        new_off[2],
    )


def solution(mesh):
    return jax.shard_map(
        body,
        mesh=mesh,
        in_specs=(
            P("dp", None, "tensor"),
            P(),
            P(),
            P("dp", "tensor"),
            P("dp", "tensor"),
            P("dp", "tensor"),
            P("dp", None, "tensor"),
            P("dp", None, "tensor"),
            P("dp", None, "tensor"),
        ),
        out_specs=(
            P(None, "tensor"),
            P(),
            P("dp", "tensor"),
            P("dp", "tensor"),
            P("dp", "tensor"),
            P("dp", None, "tensor"),
            P("dp", None, "tensor"),
            P("dp", None, "tensor"),
        ),
        check_vma=False,
    )
```

profile of v0, /device:TPU:0, one launch (start us, length us, event | category | flops | bytes accessed | tf_op | source)
XLA Modules:
  0.0 106.5 jit_solution(14819365956823482855)
XLA Ops:
  0.6 0.9 convert_reduce_fusion
  1.6 0.7 iota_compare_fusion.2
  2.6 0.7 fusion.16
  3.3 0.8 reduce_window_sum.11
  4.1 0.7 iota_subtract_fusion
  5.1 0.6 gather_fusion
  7.0 1.1 gather_fusion.1
  8.1 0.2 convert_multiply_fusion
  8.3 26.0 %fusion = f32[8,7168]{1,0:T(8,128)S(1)} fusion(f32[56,7168]{1,0:T(8,128)S(1)} %convert_multiply_fusion), kind=kCustom, calls=%all-reduce-scatter | all-reduce-scatter fusion | flops 458753 | bytes 1835520
  34.4 1.4 %collective-permute-start = (f32[7,7168]{1,0:T(8,128)S(1)}, f32[7,7168]{1,0:T(8,128)S(1)}, u32[]{:S(2)}, u32[]{:S(2)}) collective-permute-start(f32[7,7168]{1,0:T(8,128)S(1)} %slice.53), channel_id=1, source_target_pairs={{0,1},{1,2},{2,3},{3,4},{4,5},{5,6},{6,7},{8,9},{9,10},{10,11},{11... | collective-permute-start | bytes 602120
  35.9 0.6 dynamic-slice.16
  36.5 0.2 select_reduce_fusion.1
  37.4 0.6 dynamic-slice.26
  38.7 0.4 concatenate.17
  39.1 0.7 multiply_reduce_fusion
  39.9 1.2 %fusion.15 = (bf16[2,2,7168]{2,1,0:T(2,128)(2,1)S(1)}, f32[2,2,7168]{2,1,0:T(2,128)}, f32[2,2,7168]{2,1,0:T(2,128)}, f32[2,2,7168]{2,1,0:T(2,128)}) fusion(f32[2,2,7168]{2,1,0:T(2,128)S(1)} %copy-done.1, f32[2,2,7168]{2,1,0:T(2,128)S(1)} %reshape.182, f32[2,2,7168]{2,1,0:T(2,128)S(1)} %copy-done.2, f32[2,2,7168]{2,1,0:T(2,128)S(1)} %copy-done.3, ...), kind=kLoop, calls=%fused_computation.71 | loop fusion | flops 544768 | bytes 860162 | tf_op jit(solution)/shard_map/convert_element_type | solution.py:104
  41.1 1.0 gather_fusion.2
  42.1 1.0 broadcast_select_fusion.1
  43.1 6.1 %all-to-all-start = ((bf16[8,2,7168]{2,1,0:T(2,128)(2,1)}), bf16[8,2,7168]{2,1,0:T(2,128)(2,1)S(1)}, u32[]{:S(2)}, u32[]{:S(2)}) async-start(bf16[8,2,7168]{2,1,0:T(2,128)(2,1)} %broadcast_select_fusion.1), calls=%async_computation | async-start | bytes 458752 | tf_op jit(solution)/shard_map/all_to_all | solution.py:110
  49.2 0.9 fusion.13
  50.1 41.1 %psum.7 = f32[]{:T(128)} all-reduce(f32[]{:T(128)} %get-tuple-element.64), channel_id=1, replica_groups=mesh['tensor'=4,'dp'=8] {'tensor','dp'}, use_global_device_ids=true, to_apply=%region_8.10 | all-reduce | flops 1 | bytes 8 | tf_op jit(solution)/shard_map/psum | solution.py:97
  92.0 0.6 gather_fusion.3
  92.7 11.6 %all-gather = bf16[8,5,7168]{2,1,0:T(8,128)(2,1)S(1)} all-gather(bf16[1,5,7168]{2,1,0:T(8,128)(2,1)S(1)} %select_bitcast_fusion), channel_id=1, replica_groups=mesh['tensor'=4,'dp'=8] {'dp'}, dimensions={0}, use_global_device_ids=true | all-gather | bytes 645120 | tf_op jit(solution)/shard_map/all_gather | solution.py:118
  104.3 1.1 %reshape.367 = bf16[40,7168]{1,0:T(8,128)(2,1)} reshape(bf16[8,5,7168]{2,1,0:T(8,128)(2,1)S(1)} %all-gather) | data formatting | bytes 1146880
  (66 shorter events, 2.3 us)
Async XLA Ops:
  0.6 6.4 %copy-start = (bf16[1,40,7168]{2,1,0:T(8,128)(2,1)S(1)}, bf16[1,40,7168]{2,1,0:T(8,128)(2,1)}, u32[]{:S(2)}) copy-start(bf16[1,40,7168]{2,1,0:T(8,128)(2,1)} %param.11) | copy-start | bytes 1720324
  8.3 27.6 %copy-start.7 = (s32[8]{0:T(128)S(1)}, s32[8]{0:T(128)}, u32[]{:S(2)}) copy-start(s32[8]{0:T(128)} %param.13) | copy-start | bytes 100
  8.3 29.1 %copy-start.8 = (u32[32]{0:T(128)S(1)}, u32[32]{0:T(128)}, u32[]{:S(2)}) copy-start(u32[32]{0:T(128)} %constant.288) | copy-start | bytes 388
  34.3 5.5 %copy-start.1 = (f32[2,2,7168]{2,1,0:T(2,128)S(1)}, f32[2,2,7168]{2,1,0:T(2,128)}, u32[]{:S(2)}) copy-start(f32[2,2,7168]{2,1,0:T(2,128)} %param.17) | copy-start | bytes 344068
  34.4 5.5 %copy-start.2 = (f32[2,2,7168]{2,1,0:T(2,128)S(1)}, f32[2,2,7168]{2,1,0:T(2,128)}, u32[]{:S(2)}) copy-start(f32[2,2,7168]{2,1,0:T(2,128)} %param.19) | copy-start | bytes 344068
  34.4 5.5 %copy-start.3 = (f32[2,2,7168]{2,1,0:T(2,128)S(1)}, f32[2,2,7168]{2,1,0:T(2,128)}, u32[]{:S(2)}) copy-start(f32[2,2,7168]{2,1,0:T(2,128)} %param.18) | copy-start | bytes 344068
  34.4 4.2 %collective-permute-start = (f32[7,7168]{1,0:T(8,128)S(1)}, f32[7,7168]{1,0:T(8,128)S(1)}, u32[]{:S(2)}, u32[]{:S(2)}) collective-permute-start(f32[7,7168]{1,0:T(8,128)S(1)} %slice.53), channel_id=1, source_target_pairs={{0,1},{1,2},{2,3},{3,4},{4,5},{5,6},{6,7},{8,9},{9,10},{10,11},{11... | collective-permute-start | bytes 602120
  39.0 10.2 %copy-start.4 = (f32[3,7168]{1,0:T(4,128)S(1)}, f32[3,7168]{1,0:T(4,128)}, u32[]{:S(2)}) copy-start(f32[3,7168]{1,0:T(4,128)} %param.14) | copy-start | bytes 258052
  39.0 10.2 %copy-start.5 = (f32[3,7168]{1,0:T(4,128)S(1)}, f32[3,7168]{1,0:T(4,128)}, u32[]{:S(2)}) copy-start(f32[3,7168]{1,0:T(4,128)} %param.15) | copy-start | bytes 258052
  39.0 10.2 %copy-start.6 = (f32[3,7168]{1,0:T(4,128)S(1)}, f32[3,7168]{1,0:T(4,128)}, u32[]{:S(2)}) copy-start(f32[3,7168]{1,0:T(4,128)} %param.16) | copy-start | bytes 258052
  43.1 48.8 %all-to-all-start = ((bf16[8,2,7168]{2,1,0:T(2,128)(2,1)}), bf16[8,2,7168]{2,1,0:T(2,128)(2,1)S(1)}, u32[]{:S(2)}, u32[]{:S(2)}) async-start(bf16[8,2,7168]{2,1,0:T(2,128)(2,1)} %broadcast_select_fusion.1), calls=%async_computation | async-start | bytes 458752 | tf_op jit(solution)/shard_map/all_to_all | solution.py:110
where the time goes:
time: 107 us
  blocking collectives  78.7 us (74%)
  other arithmetic  8.58 us (8%)
  starting transfers between devices  7.55 us (7%)
  local copies, waits for them, and re-layouts  7.5 us (7%)
  between operations  4.15 us (4%)
    psum x1, blocking collectives, body(): grad_norm = jnp.sqrt(lax.psum(partial_value, ('tensor', 'dp')))  41.1 us
    unnamed x1, blocking collectives  26 us
    all_gather x1, blocking collectives, body(): lax.all_gather(jnp.take(stacked, order_rows, axis=0), 'dp', axis=0, tiled...  11.6 us
    all_to_all x1, starting transfers between devices, body(): lax.all_to_all(back_out, 'dp', split_axis=0, concat_axis=0, tiled=True)  6.12 us
    unnamed x23, local copies, waits for them, and re-layouts  2.18 us
  transfers between devices with their start and end apart: 2, of which 0 were waited for; matrix products, arithmetic and copies ran while one was open for 2% of the time, Pallas kernels for 0%

commit v1 on v0

--- a/solution.py
+++ b/solution.py
@@ -1,3 +1,4 @@
+import functools
 import jax
 import jax.numpy as jnp
 from jax import lax
@@ -11,6 +12,19 @@
 step_count = 10
 bias_first = 1.0 - beta_first**step_count
 bias_second = 1.0 - beta_second**step_count
+
+
+def handle_array(frame_in, net_axis):
+    fresh = jnp.concatenate(
+        lax.all_to_all(
+            jnp.stack([frame_in for _ in range(lax.psum(1, net_axis))], 0), net_axis, 0, 0
+        ),
+        0,
+    )
+    return fresh
+
+
+run_watch = functools.partial(handle_array, net_axis="dp")
 
 
 def adam_update(master, moment, second, gradient):
@@ -115,7 +129,7 @@
         kept_count + jnp.take(off_rank, position, axis=0),
         jnp.take(keep_rank, position, axis=0),
     )
-    new_weights = lax.all_gather(jnp.take(stacked, order_rows, axis=0), "dp", axis=0, tiled=True)
+    new_weights = run_watch(jnp.take(stacked, order_rows, axis=0))
     return (
         new_weights,
         grad_norm,

time: 107 us -> 112 us (1.047)
  waiting for transfers between devices: 0.01 us -> 5.64 us
  blocking collectives: 78.7 us -> 73.3 us
  starting transfers between devices: 7.55 us -> 11.1 us
    all_gather x1 -> x0, blocking collectives: 11.6 us -> none  [body(): lax.all_gather(jnp.take(stacked, order_rows, axis=0), 'dp', axis=0, tiled...]
    psum x1, blocking collectives: 41.1 us -> 47.3 us  [body(): grad_norm = jnp.sqrt(lax.psum(partial_value, ('tensor', 'dp')))]
    all_to_all x1, waiting for transfers between devices: 0.01 us -> 5.63 us  [body(): lax.all_to_all(back_out, 'dp', split_axis=0, concat_axis=0, tiled=True)]
    all_to_all x0 -> x1, starting transfers between devices: none -> 3.55 us  [handle_array(): lax.all_to_all(jnp.stack([frame_in for _ in range(lax.psum(1, net_axis))]...]
  transfers between devices with their start and end apart: 2 -> 3, of which waited for: 0 -> 1; matrix products, arithmetic and copies ran while one was open for 2% -> 2% of each run, Pallas kernels for 0% -> 0%
where the time goes in v1:
time: 112 us; the launch traced here: 111 us
  blocking collectives  73.3 us (65%)
  starting transfers between devices  11.1 us (10%)
  other arithmetic  8.57 us (8%)
  local copies, waits for them, and re-layouts  8.49 us (8%)
  waiting for transfers between devices  5.64 us (5%)
  between operations  4.14 us (4%)
    psum x1, blocking collectives, body(): grad_norm = jnp.sqrt(lax.psum(partial_value, ('tensor', 'dp')))  47.3 us
    unnamed x1, blocking collectives  26 us
    all_to_all x1, starting transfers between devices, body(): lax.all_to_all(back_out, 'dp', split_axis=0, concat_axis=0, tiled=True)  6.13 us
    all_to_all x1, waiting for transfers between devices, body(): lax.all_to_all(back_out, 'dp', split_axis=0, concat_axis=0, tiled=True)  5.63 us
    all_to_all x1, starting transfers between devices, handle_array(): lax.all_to_all(jnp.stack([frame_in for _ in range(lax.psum(1, net_axis))]...  3.55 us
  transfers between devices with their start and end apart: 3, of which 1 were waited for; matrix products, arithmetic and copies ran while one was open for 2% of the time, Pallas kernels for 0%

profile of v1, /device:TPU:0, one launch (start us, length us, event | category | flops | bytes accessed | tf_op | source)
XLA Modules:
  0.0 111.3 jit_solution(13649930519242615180)
XLA Ops:
  0.7 0.9 convert_reduce_fusion
  1.6 0.7 iota_compare_fusion.2
  2.7 0.7 fusion.16
  3.8 0.8 reduce_window_sum.11
  4.7 0.7 iota_subtract_fusion
  5.6 0.6 gather_fusion
  7.0 1.1 gather_fusion.1
  8.3 26.0 %fusion = f32[8,7168]{1,0:T(8,128)S(1)} fusion(f32[56,7168]{1,0:T(8,128)S(1)} %convert_multiply_fusion), kind=kCustom, calls=%all-reduce-scatter | all-reduce-scatter fusion | flops 458753 | bytes 1835520
  34.4 1.4 %collective-permute-start = (f32[7,7168]{1,0:T(8,128)S(1)}, f32[7,7168]{1,0:T(8,128)S(1)}, u32[]{:S(2)}, u32[]{:S(2)}) collective-permute-start(f32[7,7168]{1,0:T(8,128)S(1)} %slice.53), channel_id=1, source_target_pairs={{0,1},{1,2},{2,3},{3,4},{4,5},{5,6},{6,7},{8,9},{9,10},{10,11},{11... | collective-permute-start | bytes 602120
  35.9 0.6 dynamic-slice.16
  37.4 0.6 dynamic-slice.26
  38.6 0.4 concatenate.17
  39.0 0.7 multiply_reduce_fusion
  39.9 1.2 %fusion.15 = (bf16[2,2,7168]{2,1,0:T(2,128)(2,1)S(1)}, f32[2,2,7168]{2,1,0:T(2,128)}, f32[2,2,7168]{2,1,0:T(2,128)}, f32[2,2,7168]{2,1,0:T(2,128)}) fusion(f32[2,2,7168]{2,1,0:T(2,128)S(1)} %copy-done.1, f32[2,2,7168]{2,1,0:T(2,128)S(1)} %reshape.193, f32[2,2,7168]{2,1,0:T(2,128)S(1)} %copy-done.2, f32[2,2,7168]{2,1,0:T(2,128)S(1)} %copy-done.3, ...), kind=kLoop, calls=%fused_computation.71 | loop fusion | flops 544768 | bytes 860162 | tf_op jit(solution)/shard_map/convert_element_type | solution.py:118
  41.0 1.0 gather_fusion.2
  42.1 1.0 broadcast_select_fusion.1
  43.0 6.1 %all-to-all-start = ((bf16[8,2,7168]{2,1,0:T(2,128)(2,1)}), bf16[8,2,7168]{2,1,0:T(2,128)(2,1)S(1)}, u32[]{:S(2)}, u32[]{:S(2)}) async-start(bf16[8,2,7168]{2,1,0:T(2,128)(2,1)} %broadcast_select_fusion.1), calls=%async_computation | async-start | bytes 458752 | tf_op jit(solution)/shard_map/all_to_all | solution.py:124
  49.2 0.9 fusion.13
  50.1 5.6 %all-to-all-done = bf16[8,2,7168]{2,1,0:T(2,128)(2,1)S(1)} async-done(((bf16[8,2,7168]{2,1,0:T(2,128)(2,1)}), bf16[8,2,7168]{2,1,0:T(2,128)(2,1)S(1)}, u32[]{:S(2)}, u32[]{:S(2)}) %all-to-all-start) | async-done | bytes 229408 | tf_op jit(solution)/shard_map/all_to_all | solution.py:124
  55.8 0.6 gather_fusion.3
  56.5 1.0 stack.2
  57.5 3.6 %all-to-all-start.1 = ((bf16[8,5,7168]{2,1,0:T(8,128)(2,1)}), bf16[8,5,7168]{2,1,0:T(8,128)(2,1)S(1)}, u32[]{:S(2)}, u32[]{:S(2)}) async-start(bf16[8,5,7168]{2,1,0:T(8,128)(2,1)} %stack.2), calls=%async_computation.1 | async-start | bytes 1835008 | tf_op jit(solution)/shard_map/all_to_all | solution.py:19
  61.1 47.3 %psum.7 = f32[]{:T(128)} all-reduce(f32[]{:T(128)} %get-tuple-element.64), channel_id=1, replica_groups=mesh['tensor'=4,'dp'=8] {'tensor','dp'}, use_global_device_ids=true, to_apply=%region_8.10 | all-reduce | flops 1 | bytes 8 | tf_op jit(solution)/shard_map/psum | solution.py:111
  109.1 1.1 reshape.194
  (68 shorter events, 2.7 us)
Async XLA Ops:
  0.6 6.4 %copy-start = (bf16[1,40,7168]{2,1,0:T(8,128)(2,1)S(1)}, bf16[1,40,7168]{2,1,0:T(8,128)(2,1)}, u32[]{:S(2)}) copy-start(bf16[1,40,7168]{2,1,0:T(8,128)(2,1)} %param.11) | copy-start | bytes 1720324
  8.3 27.6 %copy-start.7 = (s32[8]{0:T(128)S(1)}, s32[8]{0:T(128)}, u32[]{:S(2)}) copy-start(s32[8]{0:T(128)} %param.13) | copy-start | bytes 100
  8.3 29.1 %copy-start.8 = (u32[32]{0:T(128)S(1)}, u32[32]{0:T(128)}, u32[]{:S(2)}) copy-start(u32[32]{0:T(128)} %constant.288) | copy-start | bytes 388
  34.3 5.5 %copy-start.1 = (f32[2,2,7168]{2,1,0:T(2,128)S(1)}, f32[2,2,7168]{2,1,0:T(2,128)}, u32[]{:S(2)}) copy-start(f32[2,2,7168]{2,1,0:T(2,128)} %param.17) | copy-start | bytes 344068
  34.4 5.5 %copy-start.2 = (f32[2,2,7168]{2,1,0:T(2,128)S(1)}, f32[2,2,7168]{2,1,0:T(2,128)}, u32[]{:S(2)}) copy-start(f32[2,2,7168]{2,1,0:T(2,128)} %param.19) | copy-start | bytes 344068
  34.4 5.5 %copy-start.3 = (f32[2,2,7168]{2,1,0:T(2,128)S(1)}, f32[2,2,7168]{2,1,0:T(2,128)}, u32[]{:S(2)}) copy-start(f32[2,2,7168]{2,1,0:T(2,128)} %param.18) | copy-start | bytes 344068
  34.4 4.2 %collective-permute-start = (f32[7,7168]{1,0:T(8,128)S(1)}, f32[7,7168]{1,0:T(8,128)S(1)}, u32[]{:S(2)}, u32[]{:S(2)}) collective-permute-start(f32[7,7168]{1,0:T(8,128)S(1)} %slice.53), channel_id=1, source_target_pairs={{0,1},{1,2},{2,3},{3,4},{4,5},{5,6},{6,7},{8,9},{9,10},{10,11},{11... | collective-permute-start | bytes 602120
  39.0 10.2 %copy-start.4 = (f32[3,7168]{1,0:T(4,128)S(1)}, f32[3,7168]{1,0:T(4,128)}, u32[]{:S(2)}) copy-start(f32[3,7168]{1,0:T(4,128)} %param.14) | copy-start | bytes 258052
  39.0 10.2 %copy-start.5 = (f32[3,7168]{1,0:T(4,128)S(1)}, f32[3,7168]{1,0:T(4,128)}, u32[]{:S(2)}) copy-start(f32[3,7168]{1,0:T(4,128)} %param.15) | copy-start | bytes 258052
  39.0 10.2 %copy-start.6 = (f32[3,7168]{1,0:T(4,128)S(1)}, f32[3,7168]{1,0:T(4,128)}, u32[]{:S(2)}) copy-start(f32[3,7168]{1,0:T(4,128)} %param.16) | copy-start | bytes 258052
  43.0 12.7 %all-to-all-start = ((bf16[8,2,7168]{2,1,0:T(2,128)(2,1)}), bf16[8,2,7168]{2,1,0:T(2,128)(2,1)S(1)}, u32[]{:S(2)}, u32[]{:S(2)}) async-start(bf16[8,2,7168]{2,1,0:T(2,128)(2,1)} %broadcast_select_fusion.1), calls=%async_computation | async-start | bytes 458752 | tf_op jit(solution)/shard_map/all_to_all | solution.py:124
  57.5 51.6 %all-to-all-start.1 = ((bf16[8,5,7168]{2,1,0:T(8,128)(2,1)}), bf16[8,5,7168]{2,1,0:T(8,128)(2,1)S(1)}, u32[]{:S(2)}, u32[]{:S(2)}) async-start(bf16[8,5,7168]{2,1,0:T(8,128)(2,1)} %stack.2), calls=%async_computation.1 | async-start | bytes 1835008 | tf_op jit(solution)/shard_map/all_to_all | solution.py:19
